TPU v7x, 32 devices: a whole 2x2x4 slice. The times are simulated.
32 devices in a mesh: ta: 4 (over x, core), ha: 4 (over z), wa: 2 (over y).
Axes of the slice: x: 2, y: 2, z: 4, core: 2. Of those that a mesh axis runs over, the one named last changes fastest.
Arguments:
- tokens: bfloat16 [1, 16, 32, 16, 1024], P(None, 'ta', 'ha', 'wa'), may hold values from -40 to 40
- norm_gain: float32 [4, 1024], replicated, may hold values from 0.25 to 1.75
- qkv_weight: bfloat16 [3, 1024, 3, 1024], P(None, None, None, 'ta'), may hold values from -0.1875 to 0.1875
- qk_gain: float32 [3, 2, 64], replicated, may hold values from 0.25 to 1.75
- out_weight: bfloat16 [3, 1024, 1024], P(None, 'ta'), may hold values from -0.1875 to 0.1875
- ffn_in: bfloat16 [1024, 2, 2048], P(None, None, 'ta'), may hold values from -0.1875 to 0.1875
- ffn_out: bfloat16 [2048, 1024], P('ta'), may hold values from -0.125 to 0.125
Outputs:
- layer_out: bfloat16 [1, 16, 32, 16, 1024], P(None, 'ta', 'ha', 'wa')
All inputs are finite; a program needn't handle non-finite values.
Results may differ from a plain program's by a relative error of at most 0.015.
Values may be sent and summed in bfloat16 or wider, within the bound.
A program may use at most 192 MiB of HBM per device.

v0:
```python
import functools

import jax
import jax.numpy as jnp
from jax import lax
from jax.experimental import pallas as pl
from jax.experimental.pallas import tpu as pltpu
from jax.sharding import PartitionSpec as P

HEAD_DIM = 64
CHUNKS = 2
EPS = 1e-06
MESH = pl.DeviceIdType.MESH
F32 = jnp.float32
BF16 = jnp.bfloat16


def dot(a, b):
    return jnp.dot(a, b, preferred_element_type=F32)


def dot_t(a, b):
    return lax.dot_general(a, b, (((1,), (1,)), ((), ())), preferred_element_type=F32)


def attend(queries, key_rows, values, mask):
    width = queries.shape[-1]
    lane_head = lax.broadcasted_iota(jnp.int32, (1, width), 1) // HEAD_DIM
    total = None
    for head in range(width // HEAD_DIM):
        pick = (lane_head == head).astype(F32).astype(BF16)
        scores = dot_t(queries * pick, key_rows)
        weights = jnp.where(mask, jnp.exp(scores), 0.0)
        probs = weights * (1.0 / jnp.sum(weights, axis=-1, keepdims=True))
        part = dot(probs.astype(BF16), values * pick)
        total = part if total is None else total + part
    return total.astype(BF16)


class Plan:
    def __init__(self, n, n_ta, frames, rows):
        self.n = n
        self.m = frames
        self.unit = rows // frames
        self.low = min(n, frames)
        self.q = frames // self.low
        self.blocks = n_ta * frames // max(n, frames)
        self.u = self.blocks * self.q


def kernel(cfg, tok, gain, qkg, wq_h, wo_h, wi_h, wf_h, out, *s):
    n_ta, frames, height, width, plans = cfg
    (stream, gath, wq, wo, wi, wf, pk, a0, a1, res0, res1, att, pk2, att2, pbuf, prec, comb, xrec,
     wsem, ag_s, ag_r, s10, r10, s20, r20, s11, r11, s21, r21, rs_s, rs_r) = s
    rows = tok.shape[0]
    per_frame = height * width
    aw = wo.shape[1]
    me = lax.axis_index("ta")
    core, chip = lax.rem(me, 2), lax.div(me, 2)

    def block_at(k):
        return lax.rem(chip + lax.div(k, 2), 2) * 2 + lax.rem(core + lax.rem(k, 2), 2)

    piece = rows // CHUNKS
    wide = lambda c: pl.ds(pl.multiple_of(c * piece, piece), piece)
    steps = n_ta * CHUNKS
    early = 2 * CHUNKS

    def arrival(i):
        late = i - early
        k = jnp.where(i < early, lax.div(i, CHUNKS), 2 + lax.rem(late, 2))
        c = jnp.where(i < early, lax.rem(i, CHUNKS), lax.div(late, 2))
        return k, c

    def departure(i):
        rest = i - early
        k = jnp.where(i < early, 3 - lax.rem(i, 2), 1 - lax.div(rest, CHUNKS))
        c = jnp.where(i < early, lax.div(i, 2), lax.rem(rest, CHUNKS))
        return k, c

    partner = block_at(1)
    remote = block_at(2)
    pair_last = block_at(3)

    copies = []
    for at in range(3):
        copies.append([
            pltpu.make_async_copy(wq_h.at[at, j], wq.at[at, :, j * aw:(j + 1) * aw], wsem.at[at, j])
            for j in range(3)])
        copies.append([pltpu.make_async_copy(wo_h.at[at], wo.at[at], wsem.at[at, 3])])
    copies.append([pltpu.make_async_copy(wi_h, wi, wsem.at[3, 0])])
    copies.append([pltpu.make_async_copy(wf_h, wf, wsem.at[3, 1])])
    for group in copies:
        for copy in group:
            copy.start()

    def ready(at):
        for copy in copies[at]:
            copy.wait()

    barrier = pltpu.get_barrier_semaphore()
    greets = 0
    for other in (partner, remote):
        pl.semaphore_signal(barrier, inc=1, device_id={"ta": other}, device_id_type=MESH)
        greets += 1
    for axis, plan in plans:
        here = lax.axis_index(axis)
        for step in range(1, plan.n):
            other = lax.rem(here + step, plan.n)
            pl.semaphore_signal(barrier, inc=1, device_id={axis: other}, device_id_type=MESH)
            greets += 1

    def remote_copy(src, dst, send, recv, axis, other):
        return pltpu.make_async_remote_copy(
            src_ref=src, dst_ref=dst, send_sem=send, recv_sem=recv,
            device_id={axis: other}, device_id_type=MESH)

    def norm_own(p, c):
        x = stream[wide(c), :]
        scale = lax.rsqrt(jnp.mean(x * x, axis=-1, keepdims=True) + EPS)
        gath[p, me, wide(c)] = (x * scale * gain[p:p + 1, :]).astype(BF16)

    def ag_copy(p, slot, c):
        block = me if slot < 2 else remote
        other = remote if slot == 1 else partner
        ref = gath.at[p, block, wide(c)]
        return remote_copy(ref, ref, ag_s.at[p, slot, c], ag_r.at[p, slot, c], "ta", other)

    def ag_start(p, c):
        ag_copy(p, 1, c).start()
        ag_copy(p, 0, c).start()

    def ag_wait(p, k, c):
        @pl.when(k == 1)
        def _():
            ag_copy(p, 0, c).wait_recv()

        @pl.when(k == 2)
        def _():
            ag_copy(p, 1, c).wait_recv()
            ag_copy(p, 2, c).start()

        @pl.when(k == 3)
        def _():
            ag_copy(p, 2, c).wait_recv()

    lane_a = lax.broadcasted_iota(jnp.int32, (aw, aw), 0) // HEAD_DIM
    lane_b = lax.broadcasted_iota(jnp.int32, (aw, aw), 1) // HEAD_DIM
    ones = (lane_a == lane_b).astype(F32).astype(BF16)

    def head_norm(x, row):
        square = x * x
        high = square.astype(BF16)
        low = (square - high.astype(F32)).astype(BF16)
        mean = (dot(high, ones) + dot(low, ones)) * (1.0 / HEAD_DIM)
        return x * lax.rsqrt(mean + EPS) * qkg[row:row + 1, :]

    def project(p, b, c):
        flat = dot(gath[p, b, wide(c)], wq[p])
        queries = (head_norm(flat[:, :aw], 2 * p) * (HEAD_DIM ** -0.5)).astype(BF16)
        key_rows = head_norm(flat[:, aw:2 * aw], 2 * p + 1).astype(BF16)
        return queries, key_rows, flat[:, 2 * aw:].astype(BF16)

    def rs_copy(p, slot, c):
        send, recv = rs_s.at[p, slot, c], rs_r.at[p, slot, c]
        if slot == 2:
            return remote_copy(comb.at[p, wide(c)], xrec.at[p, wide(c)], send, recv, "ta", remote)
        return remote_copy(pbuf.at[p, 2 * slot + 1, wide(c)], prec.at[p, slot, wide(c)], send, recv, "ta", partner)

    def rs_put(p, k, c, part):
        pbuf[p, k, wide(c)] = part.astype(BF16)

        @pl.when(k == 1)
        def _():
            rs_copy(p, 0, c).start()

        @pl.when(k == 3)
        def _():
            rs_copy(p, 1, c).start()

    def rs_combine(p, c):
        rs_copy(p, 1, c).wait_recv()
        comb[p, wide(c)] = (pbuf[p, 2, wide(c)].astype(F32) + prec[p, 1, wide(c)].astype(F32)).astype(BF16)
        rs_copy(p, 2, c).start()

    def rs_total(p, c):
        rs_copy(p, 0, c).wait_recv()
        near = pbuf[p, 0, wide(c)].astype(F32) + prec[p, 0, wide(c)].astype(F32)
        rs_copy(p, 2, c).wait_recv()
        return stream[wide(c), :] + (near + xrec[p, wide(c)].astype(F32))

    def turn(p):
        for c in range(CHUNKS):
            stream[wide(c), :] = rs_total(p, c)
            norm_own(p + 1, c)
            ag_start(p + 1, c)

    stream[...] = tok[...].astype(F32)
    norm_own(0, 0)
    pl.semaphore_wait(barrier, greets)
    ag_start(0, 0)
    for c in range(1, CHUNKS):
        norm_own(0, c)
        ag_start(0, c)

    sends = []
    for p in (0, 1):
        axis, plan = plans[p]
        n, m, unit, groups, low, fold, span = plan.n, plan.m, plan.unit, plan.u, plan.low, plan.q, plan.blocks
        here = lax.axis_index(axis)
        abuf, res = ((a0, res0), (a1, res1))[p]
        s1, r1, s2, r2 = ((s10, r10, s20, r20), (s11, r11, s21, r21))[p]
        ready(2 * p)

        def owner_of(b, j, m=m, low=low, span=span):
            return lax.rem(j, low) + m * lax.div(b, span)

        def place(j, unit=unit):
            return pl.ds(pl.multiple_of(j * unit, unit), unit)

        def unit_copy(b, j, p=p, axis=axis, low=low, fold=fold, span=span, here=here, abuf=abuf, s1=s1, r1=r1,
                      owner_of=owner_of, place=place):
            owner = owner_of(b, j)
            u = lax.rem(b, span) * fold + lax.div(j, low)
            return owner, u, remote_copy(
                pk.at[p, b, place(j)], abuf.at[u, here], s1.at[b, j], r1.at[u, here], axis, owner)

        def first(i, _, p=p, m=m, here=here, abuf=abuf, unit_copy=unit_copy, place=place):
            k, c = arrival(i)
            b = block_at(k)
            ag_wait(p, k, c)
            queries, key_rows, values = project(p, b, c)
            pk[p, b, wide(c), 0:aw] = queries
            pk[p, b, wide(c), aw:2 * aw] = key_rows
            pk[p, b, wide(c), 2 * aw:3 * aw] = values
            for at in range(m // CHUNKS):
                j = c * (m // CHUNKS) + at
                owner, u, copy = unit_copy(b, j)

                @pl.when(owner != here)
                def _():
                    copy.start()

                @pl.when(owner == here)
                def _():
                    abuf[u, here] = pk[p, b, place(j), :]
            return 0

        lax.fori_loop(0, steps, first, 0)

        size = n * unit
        if p == 0:
            line_of = lambda at: lax.div(lax.rem(at, unit), width)
        else:
            line_of = lambda at: lax.div(lax.rem(at, unit), per_frame) * width + lax.rem(at, width)
        mask = line_of(lax.broadcasted_iota(jnp.int32, (size, 1), 0)) == line_of(
            lax.broadcasted_iota(jnp.int32, (1, size), 1))

        def home(u, m=m, low=low, fold=fold, span=span, here=here):
            return lax.div(u, fold) + span * lax.div(here, m), lax.rem(here, low) + low * lax.rem(u, fold)

        def back_copy(u, other, p=p, axis=axis, res=res, s2=s2, r2=r2, home=home, place=place):
            b, j = home(u)
            return remote_copy(
                res.at[u, other], att.at[p, b, place(j)], s2.at[u, other], r2.at[b, j], axis, other)

        def second(i, _, p=p, axis=axis, n=n, unit=unit, fold=fold, span=span, here=here, abuf=abuf, res=res,
                   r1=r1, s1=s1, mask=mask, size=size, back_copy=back_copy, home=home, place=place):
            k, sub = arrival(i) if fold == CHUNKS else (lax.div(i, fold), lax.rem(i, fold))
            u = lax.rem(block_at(k), span) * fold + sub
            for step in range(1, n):
                source = lax.rem(here + step, n)
                remote_copy(abuf.at[u, source], abuf.at[u, source], s1.at[0, 0], r1.at[u, source],
                            axis, source).wait_recv()
            done = attend(
                abuf[u, :, :, 0:aw].reshape(size, aw),
                abuf[u, :, :, aw:2 * aw].reshape(size, aw),
                abuf[u, :, :, 2 * aw:3 * aw].reshape(size, aw),
                mask,
            )
            res[u] = done.reshape(n, unit, aw)
            for step in range(1, n):
                back_copy(u, lax.rem(here + step, n)).start()
            b, j = home(u)
            att[p, b, place(j)] = res[u, here]
            return 0

        lax.fori_loop(0, groups, second, 0)
        ready(2 * p + 1)

        def third(i, _, p=p, axis=axis, m=m, here=here, s2=s2, r2=r2, owner_of=owner_of, place=place):
            k, c = departure(i)
            b = block_at(k)
            for at in range(m // CHUNKS):
                j = c * (m // CHUNKS) + at
                owner = owner_of(b, j)

                @pl.when(owner != here)
                def _():
                    ref = att.at[p, b, place(j)]
                    remote_copy(ref, ref, s2.at[0, 0], r2.at[b, j], axis, owner).wait_recv()
            rs_put(p, k, c, dot(att[p, b, wide(c)], wo[p]))

            @pl.when(k == 2)
            def _():
                rs_combine(p, c)
            return 0

        lax.fori_loop(0, steps, third, 0)
        turn(p)

        def drain(unit_copy=unit_copy, back_copy=back_copy, n=n, m=m, groups=groups, here=here):
            for b in range(n_ta):
                for j in range(m):
                    owner, _, copy = unit_copy(b, j)

                    @pl.when(owner != here)
                    def _():
                        copy.wait_send()
            for u in range(groups):
                for step in range(1, n):
                    back_copy(u, lax.rem(here + step, n)).wait_send()

        sends.append(drain)

    p = 2
    some_frames = frames // CHUNKS
    ready(2 * p)

    def time_first(i, _):
        k, c = arrival(i)
        b = block_at(k)
        ag_wait(p, k, c)
        queries, key_rows, values = project(p, b, c)
        at = pl.ds(b * frames + c * some_frames, some_frames)
        pk2[at, :, 0:aw] = queries.reshape(some_frames, per_frame, aw)
        pk2[at, :, aw:2 * aw] = key_rows.reshape(some_frames, per_frame, aw)
        pk2[at, :, 2 * aw:3 * aw] = values.reshape(some_frames, per_frame, aw)
        return 0

    lax.fori_loop(0, steps, time_first, 0)
    every = n_ta * frames
    some = 16
    size = every * some
    i_at = lax.broadcasted_iota(jnp.int32, (size, 1), 0)
    j_at = lax.broadcasted_iota(jnp.int32, (1, size), 1)
    causal = (lax.rem(i_at, some) == lax.rem(j_at, some)) & (lax.div(i_at, some) >= lax.div(j_at, some))

    def time_second(g, _):
        at = pl.ds(pl.multiple_of(g * some, some), some)
        done = attend(
            pk2[:, at, 0:aw].reshape(size, aw),
            pk2[:, at, aw:2 * aw].reshape(size, aw),
            pk2[:, at, 2 * aw:3 * aw].reshape(size, aw),
            causal,
        )
        att2[:, at, :] = done.reshape(every, some, aw)
        return 0

    lax.fori_loop(0, per_frame // some, time_second, 0)
    ready(2 * p + 1)

    def time_third(i, _):
        k, c = departure(i)
        b = block_at(k)
        at = pl.ds(b * frames + c * some_frames, some_frames)
        rs_put(p, k, c, dot(att2[at].reshape(piece, aw), wo[p]))

        @pl.when(k == 2)
        def _():
            rs_combine(p, c)
        return 0

    lax.fori_loop(0, steps, time_third, 0)
    turn(p)

    ready(6)
    ready(7)
    half = wf.shape[0]

    def mlp(i, _):
        k, c = arrival(i)
        b = block_at(k)
        ag_wait(3, k, c)
        both = dot(gath[3, b, wide(c)], wi[...])
        gate, up = both[:, :half], both[:, half:]
        hidden = (gate / (1.0 + jnp.exp(-gate)) * up).astype(BF16)
        rs_put(3, k, c, dot(hidden, wf[...]))

        @pl.when((k == 2) & (c > 0))
        def _():
            rs_combine(3, c - 1)
        return 0

    lax.fori_loop(0, steps, mlp, 0)
    rs_combine(3, CHUNKS - 1)
    for c in range(CHUNKS):
        out[wide(c), :] = rs_total(3, c).astype(BF16)

    for drain in sends:
        drain()
    for p in range(4):
        for slot in range(3):
            for c in range(CHUNKS):
                ag_copy(p, slot, c).wait_send()
                rs_copy(p, slot, c).wait_send()


def local(sizes, tokens, norm_gain, qkv_weight, qk_gain, out_weight, ffn_in, ffn_out):
    n_ta, n_ha, n_wa = sizes
    extent = tokens.shape
    clips, frames, height, width, model = extent
    rows = clips * frames * height * width
    aw = qkv_weight.shape[-1]
    half = ffn_in.shape[-1]
    plans = (("wa", Plan(n_wa, n_ta, frames, rows)), ("ha", Plan(n_ha, n_ta, frames, rows)))
    cfg = (n_ta, frames, height, width, plans)
    heads = aw // HEAD_DIM
    gains = jnp.tile(qk_gain.reshape(-1, HEAD_DIM), (1, heads))
    dma = pltpu.SemaphoreType.DMA
    vm = pltpu.VMEM
    scratch = [
        vm((rows, model), F32),
        vm((4, n_ta, rows, model), BF16),
        vm((3, model, 3 * aw), BF16),
        vm((3, aw, model), BF16),
        vm((model, 2 * half), BF16),
        vm((half, model), BF16),
        vm((2, n_ta, rows, 3 * aw), BF16),
    ]
    for width_of in (3 * aw, aw):
        for _, plan in plans:
            scratch.append(vm((plan.u, plan.n, plan.unit, width_of), BF16))
    scratch += [
        vm((2, n_ta, rows, aw), BF16),
        vm((n_ta * frames, height * width, 3 * aw), BF16),
        vm((n_ta * frames, height * width, aw), BF16),
        vm((4, n_ta, rows, model), BF16),
        vm((4, 2, rows, model), BF16),
        vm((4, rows, model), BF16),
        vm((4, rows, model), BF16),
        dma((4, 4)),
        dma((4, 3, CHUNKS)),
        dma((4, 3, CHUNKS)),
    ]
    for _, plan in plans:
        scratch += [
            dma((n_ta, plan.m)),
            dma((plan.u, plan.n)),
            dma((plan.u, plan.n)),
            dma((n_ta, plan.m)),
        ]
    scratch += [dma((4, 3, CHUNKS)), dma((4, 3, CHUNKS))]
    vmem = pl.BlockSpec(memory_space=pltpu.VMEM)
    anyw = pl.BlockSpec(memory_space=pl.ANY)
    result = pl.pallas_call(
        functools.partial(kernel, cfg),
        out_shape=jax.ShapeDtypeStruct((rows, model), BF16),
        in_specs=[vmem, vmem, vmem, anyw, anyw, anyw, anyw],
        out_specs=vmem,
        scratch_shapes=scratch,
        compiler_params=pltpu.CompilerParams(
            collective_id=0, has_side_effects=True, vmem_limit_bytes=67043328),
        name="axial_layer",
    )(
        tokens.reshape(rows, model),
        norm_gain,
        gains,
        jnp.transpose(qkv_weight, (0, 2, 1, 3)),
        out_weight,
        ffn_in.reshape(model, 2 * half),
        ffn_out,
    )
    return result.reshape(extent)


def solution(mesh):
    sizes = tuple(mesh.shape[name] for name in ("ta", "ha", "wa"))
    return jax.shard_map(
        functools.partial(local, sizes),
        mesh=mesh,
        in_specs=(
            P(None, "ta", "ha", "wa", None),
            P(),
            P(None, None, None, "ta"),
            P(),
            P(None, "ta", None),
            P(None, None, "ta"),
            P("ta", None),
        ),
        out_specs=P(None, "ta", "ha", "wa", None),
        check_vma=False,
    )
```

profile of v0, /device:TPU:0, one launch (start us, length us, event | category | flops | bytes accessed | tf_op | source)
XLA Modules:
  0.0 168.6 jit_solution(9361787357970013044)
XLA Ops:
  0.0 0.7 tile.10
  0.7 0.7 tile.12.qkg
  1.4 3.5 %copy.8 = bf16[128,8,2,512]{3,1,2,0:T(8,128)(2,1)} copy(bf16[128,8,2,512]{3,2,1,0:T(2,128)(2,1)} %bitcast.8) | data formatting | bytes 4194304
  4.9 161.9 %axial_layer.1 = bf16[256,1024]{1,0:T(8,128)(2,1)} custom-call(bf16[256,1024]{1,0:T(8,128)(2,1)} %bitcast.9, f32[4,1024]{1,0:T(4,128)} %gain.1, f32[6,256]{1,0:T(8,128)} %tile.12.qkg, bf16[3,3,1024,256]{3,2,1,0:T(8,128)(2,1)} %bitcast.6, bf16[3,256,1024]{2,1,0:T(8,128)(2,1)} %wo_h.1, bf16[1024,1024]{1,0:T(8,128)(2,1)} %bitcast.5, bf16[512,1024]{1,0:T(8,128)(2,1)} %wf_h.1), custom_call_target="tpu_custom_call" | custom-call | tf_op jit(solution)/shard_map/axial_layer/pallas_call | solution.py:456
  166.8 1.9 %copy.10 = bf16[1,4,8,8,1024]{4,3,2,1,0:T(8,128)(2,1)} copy(bf16[1,4,8,8,1024]{4,3,2,1,0:T(8,128)(2,1)} %bitcast.7) | data formatting | bytes 1048576
  (1 shorter events, 0.0 us)
where the time goes:
time: 171 us; the launch traced here: 169 us
  Pallas kernels  162 us (95%)
  local copies, waits for them, and re-layouts  6.76 us (4%)
    pallas_call x1, Pallas kernels, local(): pl.pallas_call(functools.partial(kernel, cfg), out_shape=jax.ShapeDtypeSt...  162 us
    unnamed x2, local copies, waits for them, and re-layouts  5.38 us

commit v1 on v0

--- a/solution.py
+++ b/solution.py
@@ -48,7 +48,7 @@
         self.u = self.blocks * self.q
 
 
-def kernel(cfg, tok, gain, qkg, wq_h, wo_h, wi_h, wf_h, out, *s):
+def general_kernel(cfg, tok, gain, qkg, wq_h, wo_h, wi_h, wf_h, out, *s):
     n_ta, frames, height, width, plans = cfg
     (stream, gath, wq, wo, wi, wf, pk, a0, a1, res0, res1, att, pk2, att2, pbuf, prec, comb, xrec,
      wsem, ag_s, ag_r, s10, r10, s20, r20, s11, r11, s21, r21, rs_s, rs_r) = s
@@ -406,7 +406,7 @@
                 rs_copy(p, slot, c).wait_send()
 
 
-def local(sizes, tokens, norm_gain, qkv_weight, qk_gain, out_weight, ffn_in, ffn_out):
+def general_local(sizes, tokens, norm_gain, qkv_weight, qk_gain, out_weight, ffn_in, ffn_out):
     n_ta, n_ha, n_wa = sizes
     extent = tokens.shape
     clips, frames, height, width, model = extent
@@ -454,7 +454,7 @@
     vmem = pl.BlockSpec(memory_space=pltpu.VMEM)
     anyw = pl.BlockSpec(memory_space=pl.ANY)
     result = pl.pallas_call(
-        functools.partial(kernel, cfg),
+        functools.partial(general_kernel, cfg),
         out_shape=jax.ShapeDtypeStruct((rows, model), BF16),
         in_specs=[vmem, vmem, vmem, anyw, anyw, anyw, anyw],
         out_specs=vmem,
@@ -474,6 +474,540 @@
     return result.reshape(extent)
 
 
+def axial_kernel(cfg, tok, gain, qkg, wq_h, wo_h, wi_h, wf_h, out, *s):
+    n_ta, n_ha, n_wa, frames, height, width = cfg
+    (x0, stream, gath, wq, wo, wi, wf, wi_far, wf_far, sx1, x1, pk2, att2, pbuf, prec, comb, xrec, fo, ro,
+     wsem, x0_s, x0_r, ag_s, ag_r, rs_s, rs_r, x1_s, x1_r, fo_s, fo_r,
+     wx_s, wx_r, wz_s, wz_r, wy_s, wy_r) = s
+    model = tok.shape[-1]
+    aw = wo.shape[1]
+    piece = frames * height * width // CHUNKS
+    some_frames = frames // CHUNKS
+    sub_rows = height // n_wa
+    sub_cols = width // n_ha
+    spots = sub_rows * sub_cols
+    unit = some_frames * spots
+    groups = n_ha * n_wa
+    some_groups = groups // CHUNKS
+    some_wa = n_wa // CHUNKS
+    me = lax.axis_index("ta")
+    at_ha = lax.axis_index("ha")
+    at_wa = lax.axis_index("wa")
+    here = at_wa * n_ha + at_ha
+    core, chip = lax.rem(me, 2), lax.div(me, 2)
+
+    def block_at(k):
+        return lax.rem(chip + lax.div(k, 2), 2) * 2 + lax.rem(core + lax.rem(k, 2), 2)
+
+    partner = block_at(1)
+    remote = block_at(2)
+    steps = n_ta * CHUNKS
+    early = 2 * CHUNKS
+
+    def arrival(i):
+        late = i - early
+        c = jnp.where(i < early, lax.div(i, 2), lax.div(late, 2))
+        k = jnp.where(i < early, lax.rem(i, 2), 2 + lax.rem(late, 2))
+        return k, c
+
+    copies = []
+    for at in range(3):
+        copies.append([
+            pltpu.make_async_copy(wq_h.at[at, j], wq.at[at, :, j * aw:(j + 1) * aw], wsem.at[at, j])
+            for j in range(3)])
+        copies.append([pltpu.make_async_copy(wo_h.at[at], wo.at[at], wsem.at[at, 3])])
+    copies.append([pltpu.make_async_copy(wi_h, wi, wsem.at[3, 0])])
+    copies.append([pltpu.make_async_copy(wf_h, wf, wsem.at[3, 1])])
+
+    def ready(at):
+        for copy in copies[at]:
+            copy.wait()
+
+    barrier = pltpu.get_barrier_semaphore()
+    for other in (partner, remote):
+        pl.semaphore_signal(barrier, inc=1, device_id={"ta": other}, device_id_type=MESH)
+
+    def group_place(g):
+        return {"wa": lax.div(g, n_ha), "ha": lax.rem(g, n_ha)}
+
+    for step in range(1, groups):
+        pl.semaphore_signal(barrier, inc=1, device_id=group_place(lax.rem(here + step, groups)), device_id_type=MESH)
+    greets = groups + 1
+
+    def remote_copy(src, dst, send, recv, place):
+        return pltpu.make_async_remote_copy(
+            src_ref=src, dst_ref=dst, send_sem=send, recv_sem=recv,
+            device_id=place, device_id_type=MESH)
+
+    for group in copies:
+        for copy in group:
+            copy.start()
+
+    def x0_copy(c, source, target):
+        at = pl.ds(c * some_frames, some_frames)
+        return remote_copy(tok.at[at, target], x0.at[at, source], x0_s.at[c, target], x0_r.at[c, source],
+                           {"wa": target})
+
+    far_pairs = ((wi_h, wi_far), (wf_h, wf_far))
+
+    def far_x(j):
+        src, dst = far_pairs[j]
+        size = dst.shape[2]
+        at = pl.ds(pl.multiple_of(here * size, size), size)
+        return remote_copy(src.at[at], dst.at[at_wa, at_ha], wx_s.at[j], wx_r.at[j], {"ta": remote})
+
+    def far_z(j, source, target):
+        ref = far_pairs[j][1].at[at_wa, source]
+        return remote_copy(ref, ref, wz_s.at[j, target], wz_r.at[j, source], {"ha": target})
+
+    def far_y(j, wa_source, part, target):
+        ref = far_pairs[j][1].at[wa_source, part]
+        return remote_copy(ref, ref, wy_s.at[j, target, part], wy_r.at[j, wa_source, part], {"wa": target})
+
+    def far_spread(part):
+        for j in range(2):
+            for step in range(1, n_wa):
+                far_y(j, at_wa, part, lax.rem(at_wa + step, n_wa)).start()
+
+    def far_first():
+        for j in range(2):
+            far_x(j).wait_recv()
+            for step in range(1, n_ha):
+                far_z(j, at_ha, lax.rem(at_ha + step, n_ha)).start()
+        far_spread(at_ha)
+
+    def far_next(step):
+        source = lax.rem(at_ha + step, n_ha)
+        for j in range(2):
+            far_z(j, source, source).wait_recv()
+        far_spread(source)
+
+    def far_ready():
+        for j in range(2):
+            for step in range(1, n_wa):
+                source = lax.rem(at_wa + step, n_wa)
+                for part in range(n_ha):
+                    far_y(j, source, part, source).wait_recv()
+
+    def norm_own(p, c):
+        x = stream[p // 2, c]
+        scale = lax.rsqrt(jnp.mean(x * x, axis=-1, keepdims=True) + EPS)
+        gath[p, me, c] = (x * scale * gain[p:p + 1, :]).astype(BF16)
+
+    def ag_copy(p, slot, c):
+        block = me if slot < 2 else remote
+        other = remote if slot == 1 else partner
+        ref = gath.at[p, block, c]
+        return remote_copy(ref, ref, ag_s.at[p, slot, c], ag_r.at[p, slot, c], {"ta": other})
+
+    def ag_start(p, c):
+        ag_copy(p, 1, c).start()
+        ag_copy(p, 0, c).start()
+
+    def ag_wait(p, k, c):
+        @pl.when(k == 1)
+        def _():
+            ag_copy(p, 0, c).wait_recv()
+
+        @pl.when(k == 2)
+        def _():
+            ag_copy(p, 1, c).wait_recv()
+            ag_copy(p, 2, c).start()
+
+        @pl.when(k == 3)
+        def _():
+            ag_copy(p, 2, c).wait_recv()
+
+    lane_a = lax.broadcasted_iota(jnp.int32, (aw, aw), 0) // HEAD_DIM
+    lane_b = lax.broadcasted_iota(jnp.int32, (aw, aw), 1) // HEAD_DIM
+    ones = (lane_a == lane_b).astype(F32).astype(BF16)
+
+    def head_norm(x, row):
+        square = x * x
+        high = square.astype(BF16)
+        low = (square - high.astype(F32)).astype(BF16)
+        mean = (dot(high, ones) + dot(low, ones)) * (1.0 / HEAD_DIM)
+        return x * lax.rsqrt(mean + EPS) * qkg[row:row + 1, :]
+
+    def project(p, b, c):
+        flat = dot(gath[p, b, c], wq[p])
+        queries = (head_norm(flat[:, :aw], 2 * p) * (HEAD_DIM ** -0.5)).astype(BF16)
+        key_rows = head_norm(flat[:, aw:2 * aw], 2 * p + 1).astype(BF16)
+        return queries, key_rows, flat[:, 2 * aw:].astype(BF16)
+
+    def rs_copy(p, slot, c):
+        send, recv = rs_s.at[p, slot, c], rs_r.at[p, slot, c]
+        if slot == 2:
+            return remote_copy(comb.at[p, c], xrec.at[p, c], send, recv, {"ta": remote})
+        return remote_copy(pbuf.at[p, 2 * slot + 1, c], prec.at[p, slot, c], send, recv, {"ta": partner})
+
+    def rs_put(p, k, c, part):
+        pbuf[p, k, c] = part.astype(BF16)
+
+        @pl.when(k == 1)
+        def _():
+            rs_copy(p, 0, c).start()
+
+        @pl.when(k == 3)
+        def _():
+            rs_copy(p, 1, c).start()
+
+    def rs_combine(p, c):
+        rs_copy(p, 1, c).wait_recv()
+        comb[p, c] = (pbuf[p, 2, c].astype(F32) + prec[p, 1, c].astype(F32)).astype(BF16)
+        rs_copy(p, 2, c).start()
+
+    def rs_near(p, c):
+        rs_copy(p, 0, c).wait_recv()
+        return pbuf[p, 0, c].astype(F32) + prec[p, 0, c].astype(F32)
+
+    def rs_total(p, c):
+        near = rs_near(p, c)
+        rs_copy(p, 2, c).wait_recv()
+        return stream[p // 2, c] + (near + xrec[p, c].astype(F32))
+
+    def pick_rows(source):
+        return (source == lax.broadcasted_iota(jnp.int32, (1, piece), 1)).astype(F32).astype(BF16)
+
+    index = lax.broadcasted_iota(jnp.int32, (piece, 1), 0)
+
+    def digits(value, sizes):
+        found = []
+        for size in sizes[::-1]:
+            found.append(lax.rem(value, size))
+            value = lax.div(value, size)
+        return found[::-1]
+
+    def number(parts, sizes):
+        value = parts[0]
+        for part, size in zip(parts[1:], sizes[1:]):
+            value = value * size + part
+        return value
+
+    def x1_copy(c, source, target):
+        return remote_copy(sx1.at[c, target], x1.at[c, source], x1_s.at[c, target], x1_r.at[c, source],
+                           group_place(target))
+
+    def x1_send(c):
+        w, h, f, r, q = digits(index, (n_wa, n_ha, some_frames, sub_rows, sub_cols))
+        source = number((f, w, r, h, q), (some_frames, n_wa, sub_rows, n_ha, sub_cols))
+        moved = dot(pick_rows(source), rs_total(0, c).astype(BF16)).astype(BF16)
+        sx1[c] = moved.reshape(groups, unit, model)
+        for step in range(1, groups):
+            x1_copy(c, here, lax.rem(here + step, groups)).start()
+        x1[c, here] = sx1[c, here]
+
+    def x1_take(c):
+        for step in range(1, groups):
+            source = lax.rem(here + step, groups)
+            x1_copy(c, source, source).wait_recv()
+        stream[0, c] = x1[c].reshape(piece, model).astype(F32)
+        norm_own(1, c)
+        ag_start(1, c)
+
+    def fo_copy(c, source, target):
+        return remote_copy(fo.at[c, :, :, target], ro.at[c, source], fo_s.at[c, target], fo_r.at[c, source],
+                           {"ha": target})
+
+    def fo_send(c):
+        near = rs_near(3, c)
+        total = (stream[1, c] + near).astype(BF16)
+        fo[c] = total.reshape(CHUNKS, some_wa, n_ha, unit, model)
+        for step in range(1, n_ha):
+            fo_copy(c, at_ha, lax.rem(at_ha + step, n_ha)).start()
+        ro[c, at_ha] = fo[c, :, :, at_ha]
+
+    def fo_take(c):
+        for step in range(1, n_ha):
+            source = lax.rem(at_ha + step, n_ha)
+            fo_copy(c, source, source).wait_recv()
+        f0, f1, w, r, h, q = digits(index, (CHUNKS, some_frames, some_wa, sub_rows, n_ha, sub_cols))
+        source = number((h, f0, w, f1, r, q), (n_ha, CHUNKS, some_wa, some_frames, sub_rows, sub_cols))
+        moved = dot(pick_rows(source), ro[c].reshape(piece, model)).astype(BF16)
+        out[:, c * some_wa:(c + 1) * some_wa] = moved.reshape(frames, some_wa, sub_rows * width, model)
+
+    x0[:, at_wa] = tok[:, at_wa]
+    pl.semaphore_wait(barrier, greets)
+    for c in range(CHUNKS):
+        for step in range(1, n_wa):
+            x0_copy(c, at_wa, lax.rem(at_wa + step, n_wa)).start()
+    for j in range(2):
+        far_x(j).start()
+    for c in range(CHUNKS):
+        for step in range(1, n_wa):
+            source = lax.rem(at_wa + step, n_wa)
+            x0_copy(c, source, source).wait_recv()
+        stream[0, c] = x0[c * some_frames:(c + 1) * some_frames].reshape(piece, model).astype(F32)
+        norm_own(0, c)
+        ag_start(0, c)
+
+    column = lax.broadcasted_iota(jnp.int32, (1, piece), 1)
+
+    def lines_0(at):
+        f, w, r, q = digits(at, (some_frames, n_wa, sub_rows, width))
+        return f * sub_rows + r
+
+    def lines_1(at):
+        g, f, r, q = digits(at, (groups, some_frames, sub_rows, sub_cols))
+        return f * sub_cols + q
+
+    def line_step(p, i, mask):
+        k, c = arrival(i)
+        b = block_at(k)
+        ag_wait(p, k, c)
+        queries, key_rows, values = project(p, b, c)
+        rs_put(p, k, c, dot(attend(queries, key_rows, values, mask), wo[p]))
+
+        @pl.when((k == 2) & (c > 0))
+        def _():
+            rs_combine(p, c - 1)
+
+    ready(0)
+    ready(1)
+    mask_0 = lines_0(index) == lines_0(column)
+
+    def pass_0(i, _):
+        line_step(0, i, mask_0)
+        return 0
+
+    lax.fori_loop(0, steps, pass_0, 0)
+    rs_combine(0, CHUNKS - 1)
+    far_first()
+    x1_send(0)
+    x1_take(0)
+    ready(2)
+    ready(3)
+    mask_1 = lines_1(index) == lines_1(column)
+
+    def pass_1(i, _):
+        for c in range(1, CHUNKS):
+            @pl.when(i == 2 * c - 1)
+            def _():
+                x1_send(c)
+
+            @pl.when(i == 2 * c)
+            def _():
+                x1_take(c)
+
+        line_step(1, i, mask_1)
+        return 0
+
+    lax.fori_loop(0, steps, pass_1, 0)
+    rs_combine(1, CHUNKS - 1)
+    far_next(1)
+
+    half_piece = piece // CHUNKS
+    for c in range(CHUNKS):
+        total = rs_total(1, c)
+        for d in range(CHUNKS):
+            stream[1, d, c * half_piece:(c + 1) * half_piece] = total[d * half_piece:(d + 1) * half_piece]
+    for d in range(CHUNKS):
+        norm_own(2, d)
+        ag_start(2, d)
+
+    for at in (4, 5):
+        ready(at)
+    for step in range(2, n_ha):
+        far_next(step)
+    t_i = lax.div(index, unit) * some_frames + lax.div(lax.rem(index, unit), spots)
+    t_j = lax.div(column, unit) * some_frames + lax.div(lax.rem(column, unit), spots)
+    causal = (lax.rem(index, spots) == lax.rem(column, spots)) & (t_i >= t_j)
+
+    def time_project(i, _):
+        k, c = arrival(i)
+        b = block_at(k)
+        ag_wait(2, k, c)
+        queries, key_rows, values = project(2, b, c)
+        pk2[c, b, :, :, :, 0:aw] = queries.reshape(CHUNKS, some_groups, unit, aw)
+        pk2[c, b, :, :, :, aw:2 * aw] = key_rows.reshape(CHUNKS, some_groups, unit, aw)
+        pk2[c, b, :, :, :, 2 * aw:3 * aw] = values.reshape(CHUNKS, some_groups, unit, aw)
+        return 0
+
+    def time_attend(i, _):
+        c = lax.div(i, some_groups)
+        g = lax.rem(i, some_groups)
+        done = attend(
+            pk2[c, :, :, g, :, 0:aw].reshape(piece, aw),
+            pk2[c, :, :, g, :, aw:2 * aw].reshape(piece, aw),
+            pk2[c, :, :, g, :, 2 * aw:3 * aw].reshape(piece, aw),
+            causal,
+        )
+        att2[c, :, :, g] = done.reshape(n_ta, CHUNKS, unit, aw)
+        return 0
+
+    def time_out(i, _):
+        c = lax.div(i, n_ta)
+        k = 3 - lax.rem(i, n_ta)
+        b = block_at(k)
+        rs_put(2, k, c, dot(att2[c, b].reshape(piece, aw), wo[2]))
+
+        @pl.when(k == 1)
+        def _():
+            rs_combine(2, c)
+        return 0
+
+    lax.fori_loop(0, early, time_project, 0)
+
+    def time_chunk(c, _):
+        lax.fori_loop(early + 2 * c, early + 2 * c + 2, time_project, 0)
+        lax.fori_loop(c * some_groups, (c + 1) * some_groups, time_attend, 0)
+        lax.fori_loop(c * n_ta, (c + 1) * n_ta, time_out, 0)
+        return 0
+
+    lax.fori_loop(0, CHUNKS, time_chunk, 0)
+
+    for at in (6, 7):
+        ready(at)
+    far_ready()
+    half = wf.shape[0]
+
+    def silu_part(x, w_in, w_out):
+        both = dot(x, w_in)
+        gate, up = both[:, :half], both[:, half:]
+        hidden = (gate / (1.0 + jnp.exp(-gate)) * up).astype(BF16)
+        return dot(hidden, w_out)
+
+    def mlp(i, _):
+        k, c = lax.rem(i, 2), lax.div(i, 2)
+        b = block_at(k)
+
+        for d in range(CHUNKS):
+            @pl.when(i == 2 * d)
+            def _():
+                stream[1, d] = rs_total(2, d)
+                norm_own(3, d)
+                ag_copy(3, 0, d).start()
+
+        @pl.when(k == 1)
+        def _():
+            ag_copy(3, 0, c).wait_recv()
+
+        x = gath[3, b, c]
+        part = silu_part(x, wi[...], wf[...]) + silu_part(
+            x, wi_far[...].reshape(model, 2 * half), wf_far[...].reshape(half, model))
+        pbuf[3, k, c] = part.astype(BF16)
+
+        @pl.when(k == 1)
+        def _():
+            rs_copy(3, 0, c).start()
+
+        return 0
+
+    lax.fori_loop(0, 2 * CHUNKS, mlp, 0)
+    for c in range(CHUNKS):
+        fo_send(c)
+    for c in range(CHUNKS):
+        fo_take(c)
+
+    for c in range(CHUNKS):
+        for step in range(1, n_wa):
+            x0_copy(c, at_wa, lax.rem(at_wa + step, n_wa)).wait_send()
+        for step in range(1, groups):
+            x1_copy(c, here, lax.rem(here + step, groups)).wait_send()
+        for step in range(1, n_ha):
+            fo_copy(c, at_ha, lax.rem(at_ha + step, n_ha)).wait_send()
+        for p in range(3):
+            for slot in range(3):
+                ag_copy(p, slot, c).wait_send()
+                rs_copy(p, slot, c).wait_send()
+        ag_copy(3, 0, c).wait_send()
+        rs_copy(3, 0, c).wait_send()
+    for j in range(2):
+        far_x(j).wait_send()
+        for step in range(1, n_ha):
+            far_z(j, at_ha, lax.rem(at_ha + step, n_ha)).wait_send()
+        for step in range(1, n_wa):
+            for part in range(n_ha):
+                far_y(j, at_wa, part, lax.rem(at_wa + step, n_wa)).wait_send()
+
+
+def axial_local(sizes, tokens, norm_gain, qkv_weight, qk_gain, out_weight, ffn_in, ffn_out):
+    n_ta, n_ha, n_wa = sizes
+    extent = tokens.shape
+    clips, frames, height, width, model = extent
+    frames = clips * frames
+    rows = frames * height * width
+    piece = rows // CHUNKS
+    aw = qkv_weight.shape[-1]
+    half = ffn_in.shape[-1]
+    groups = n_ha * n_wa
+    unit = piece // groups
+    sub = height // n_wa * width
+    heads = aw // HEAD_DIM
+    gains = jnp.tile(qk_gain.reshape(-1, HEAD_DIM), (1, heads))
+    dma = pltpu.SemaphoreType.DMA
+    vm = pltpu.VMEM
+    scratch = [
+        vm((frames, n_wa, sub, model), BF16),
+        vm((2, CHUNKS, piece, model), F32),
+        vm((4, n_ta, CHUNKS, piece, model), BF16),
+        vm((3, model, 3 * aw), BF16),
+        vm((3, aw, model), BF16),
+        vm((model, 2 * half), BF16),
+        vm((half, model), BF16),
+        vm((n_wa, n_ha, model // groups, 2 * half), BF16),
+        vm((n_wa, n_ha, half // groups, model), BF16),
+        vm((CHUNKS, groups, unit, model), BF16),
+        vm((CHUNKS, groups, unit, model), BF16),
+        vm((CHUNKS, n_ta, CHUNKS, groups // CHUNKS, unit, 3 * aw), BF16),
+        vm((CHUNKS, n_ta, CHUNKS, groups // CHUNKS, unit, aw), BF16),
+        vm((4, n_ta, CHUNKS, piece, model), BF16),
+        vm((4, 2, CHUNKS, piece, model), BF16),
+        vm((3, CHUNKS, piece, model), BF16),
+        vm((3, CHUNKS, piece, model), BF16),
+        vm((CHUNKS, CHUNKS, n_wa // CHUNKS, n_ha, unit, model), BF16),
+        vm((CHUNKS, n_ha, CHUNKS, n_wa // CHUNKS, unit, model), BF16),
+        dma((4, 4)),
+        dma((CHUNKS, n_wa)),
+        dma((CHUNKS, n_wa)),
+        dma((4, 3, CHUNKS)),
+        dma((4, 3, CHUNKS)),
+        dma((4, 3, CHUNKS)),
+        dma((4, 3, CHUNKS)),
+        dma((CHUNKS, groups)),
+        dma((CHUNKS, groups)),
+        dma((CHUNKS, n_ha)),
+        dma((CHUNKS, n_ha)),
+        dma((2,)),
+        dma((2,)),
+        dma((2, n_ha)),
+        dma((2, n_ha)),
+        dma((2, n_wa, n_ha)),
+        dma((2, n_wa, n_ha)),
+    ]
+    vmem = pl.BlockSpec(memory_space=pltpu.VMEM)
+    anyw = pl.BlockSpec(memory_space=pl.ANY)
+    result = pl.pallas_call(
+        functools.partial(axial_kernel, (n_ta, n_ha, n_wa, frames, height, width)),
+        out_shape=jax.ShapeDtypeStruct((frames, n_wa, sub, model), BF16),
+        in_specs=[vmem, vmem, vmem, anyw, anyw, anyw, anyw],
+        out_specs=vmem,
+        scratch_shapes=scratch,
+        compiler_params=pltpu.CompilerParams(
+            collective_id=0, has_side_effects=True, vmem_limit_bytes=67043328),
+        name="axial_layer",
+    )(
+        tokens.reshape(frames, n_wa, sub, model),
+        norm_gain,
+        gains,
+        jnp.transpose(qkv_weight, (0, 2, 1, 3)),
+        out_weight,
+        ffn_in.reshape(model, 2 * half),
+        ffn_out,
+    )
+    return result.reshape(extent)
+
+
+def local(sizes, tokens, *weights):
+    n_ta, n_ha, n_wa = sizes
+    clips, frames, height, width, _ = tokens.shape
+    fits = n_wa % CHUNKS == 0 and height % n_wa == 0 and width % n_ha == 0 and clips * frames % CHUNKS == 0
+    unit = clips * frames * height * width // (CHUNKS * n_ha * n_wa)
+    if fits and unit % 16 == 0:
+        return axial_local(sizes, tokens, *weights)
+    return general_local(sizes, tokens, *weights)
+
+
 def solution(mesh):
     sizes = tuple(mesh.shape[name] for name in ("ta", "ha", "wa"))
     return jax.shard_map(

time: 171 us -> 154 us (0.901); the launches traced: 169 us -> 154 us
  Pallas kernels: 162 us -> 147 us
    pallas_call x1, Pallas kernels: 162 us -> 147 us  [axial_local(): pl.pallas_call(functools.partial(axial_kernel, (n_ta, n_ha, n_wa, frames,...]
where the time goes in v1:
time: 154 us
  Pallas kernels  147 us (95%)
  local copies, waits for them, and re-layouts  6.76 us (4%)
    pallas_call x1, Pallas kernels, axial_local(): pl.pallas_call(functools.partial(axial_kernel, (n_ta, n_ha, n_wa, frames,...  147 us
    unnamed x2, local copies, waits for them, and re-layouts  5.38 us

profile of v1, /device:TPU:0, one launch (start us, length us, event | category | flops | bytes accessed | tf_op | source)
XLA Modules:
  0.0 153.8 jit_solution(8189392913719454708)
XLA Ops:
  0.0 0.7 tile.10
  0.7 0.7 tile.12.qkg
  1.4 3.5 %copy.8 = bf16[128,8,2,512]{3,1,2,0:T(8,128)(2,1)} copy(bf16[128,8,2,512]{3,2,1,0:T(2,128)(2,1)} %bitcast.8) | data formatting | bytes 4194304
  4.9 147.0 %axial_layer.1 = bf16[4,2,32,1024]{3,2,1,0:T(8,128)(2,1)} custom-call(bf16[4,2,32,1024]{3,2,1,0:T(8,128)(2,1)} %bitcast.9, f32[4,1024]{1,0:T(4,128)} %gain.1, f32[6,256]{1,0:T(8,128)} %tile.12.qkg, bf16[3,3,1024,256]{3,2,1,0:T(8,128)(2,1)} %bitcast.6, bf16[3,256,1024]{2,1,0:T(8,128)(2,1)} %wo_h.1, bf16[1024,1024]{1,0:T(8,128)(2,1)} %bitcast.5, ...), custom_call_target="tpu_custom_call" | custom-call | tf_op jit(solution)/shard_map/axial_layer/pallas_call | solution.py:980
  151.9 1.9 %copy.10 = bf16[1,4,8,8,1024]{4,3,2,1,0:T(8,128)(2,1)} copy(bf16[1,4,8,8,1024]{4,3,2,1,0:T(8,128)(2,1)} %bitcast.7) | data formatting | bytes 1048576
  (1 shorter events, 0.0 us)

commit v2 on v1

--- a/solution.py
+++ b/solution.py
@@ -476,11 +476,11 @@
 
 def axial_kernel(cfg, tok, gain, qkg, wq_h, wo_h, wi_h, wf_h, out, *s):
     n_ta, n_ha, n_wa, frames, height, width = cfg
-    (x0, stream, gath, wq, wo, wi, wf, wi_far, wf_far, sx1, x1, pk2, att2, pbuf, prec, comb, xrec, fo, ro,
-     wsem, x0_s, x0_r, ag_s, ag_r, rs_s, rs_r, x1_s, x1_r, fo_s, fo_r,
-     wx_s, wx_r, wz_s, wz_r, wy_s, wy_r) = s
+    (x0, stream, gath, wq, wo, wi, wf, wi_far, wf_far, sx1, x1, pk2, attb, att, pbuf, prec, fo, ro,
+     wsem, x0_s, x0_r, ag_s, ag_r, rs_s, rs_r, at_s, at_r, x1_s, x1_r, fo_s, fo_r,
+     wx_s, wx_r, wz_s, wz_r, wy_s, wy_r, wd_s, wd_r) = s
     model = tok.shape[-1]
-    aw = wo.shape[1]
+    aw = pk2.shape[-1] // 3
     piece = frames * height * width // CHUNKS
     some_frames = frames // CHUNKS
     sub_rows = height // n_wa
@@ -501,6 +501,7 @@
 
     partner = block_at(1)
     remote = block_at(2)
+    part_rows = piece // n_wa
     steps = n_ta * CHUNKS
     early = 2 * CHUNKS
 
@@ -515,7 +516,7 @@
         copies.append([
             pltpu.make_async_copy(wq_h.at[at, j], wq.at[at, :, j * aw:(j + 1) * aw], wsem.at[at, j])
             for j in range(3)])
-        copies.append([pltpu.make_async_copy(wo_h.at[at], wo.at[at], wsem.at[at, 3])])
+        copies.append([pltpu.make_async_copy(wo_h.at[at], wo.at[at, me], wsem.at[at, 3])])
     copies.append([pltpu.make_async_copy(wi_h, wi, wsem.at[3, 0])])
     copies.append([pltpu.make_async_copy(wf_h, wf, wsem.at[3, 1])])
 
@@ -545,78 +546,108 @@
 
     def x0_copy(c, source, target):
         at = pl.ds(c * some_frames, some_frames)
-        return remote_copy(tok.at[at, target], x0.at[at, source], x0_s.at[c, target], x0_r.at[c, source],
+        return remote_copy(tok.at[at, target], x0.at[c, source], x0_s.at[c, target], x0_r.at[c, source],
                            {"wa": target})
 
-    far_pairs = ((wi_h, wi_far), (wf_h, wf_far))
+    parts_in = wi_h.shape[0] // wi_far.shape[0]
+
+    def far(j, shard):
+        if j < 3:
+            return wo.at[j, shard]
+        return wi_far.at[j - 3] if j < 5 else wf_far
 
     def far_x(j):
-        src, dst = far_pairs[j]
-        size = dst.shape[2]
-        at = pl.ds(pl.multiple_of(here * size, size), size)
-        return remote_copy(src.at[at], dst.at[at_wa, at_ha], wx_s.at[j], wx_r.at[j], {"ta": remote})
+        dst = far(j, me).at[at_wa, at_ha]
+        if j < 3:
+            src = wo_h.at[j, at_wa, at_ha]
+        else:
+            size = dst.shape[0]
+            first = (j - 3) * parts_in if j < 5 else 0
+            src = (wi_h if j < 5 else wf_h).at[pl.ds(pl.multiple_of(first + here * size, size), size)]
+        return remote_copy(src, dst, wx_s.at[j], wx_r.at[j], {"ta": remote})
 
     def far_z(j, source, target):
-        ref = far_pairs[j][1].at[at_wa, source]
+        ref = far(j, remote).at[at_wa, source]
         return remote_copy(ref, ref, wz_s.at[j, target], wz_r.at[j, source], {"ha": target})
 
     def far_y(j, wa_source, part, target):
-        ref = far_pairs[j][1].at[wa_source, part]
+        ref = far(j, remote).at[wa_source, part]
         return remote_copy(ref, ref, wy_s.at[j, target, part], wy_r.at[j, wa_source, part], {"wa": target})
 
-    def far_spread(part):
-        for j in range(2):
-            for step in range(1, n_wa):
-                far_y(j, at_wa, part, lax.rem(at_wa + step, n_wa)).start()
-
-    def far_first():
-        for j in range(2):
-            far_x(j).wait_recv()
-            for step in range(1, n_ha):
-                far_z(j, at_ha, lax.rem(at_ha + step, n_ha)).start()
-        far_spread(at_ha)
-
-    def far_next(step):
-        source = lax.rem(at_ha + step, n_ha)
-        for j in range(2):
+    def far_d(j, slot):
+        if slot == 0:
+            return remote_copy(wo_h.at[j], wo.at[j, me], wd_s.at[j, 0], wd_r.at[j, 0], {"ta": partner})
+        ref = wo.at[j, remote]
+        return remote_copy(ref, ref, wd_s.at[j, 1], wd_r.at[j, 1], {"ta": partner})
+
+    def far_spread(j, part):
+        for step in range(1, n_wa):
+            far_y(j, at_wa, part, lax.rem(at_wa + step, n_wa)).start()
+
+    def far_first(j):
+        far_x(j).wait_recv()
+        for step in range(1, n_ha):
+            far_z(j, at_ha, lax.rem(at_ha + step, n_ha)).start()
+
+    def far_own(j):
+        far_spread(j, at_ha)
+
+    def far_next(j):
+        for step in range(1, n_ha):
+            source = lax.rem(at_ha + step, n_ha)
             far_z(j, source, source).wait_recv()
-        far_spread(source)
-
-    def far_ready():
-        for j in range(2):
-            for step in range(1, n_wa):
-                source = lax.rem(at_wa + step, n_wa)
-                for part in range(n_ha):
-                    far_y(j, source, part, source).wait_recv()
-
-    def norm_own(p, c):
-        x = stream[p // 2, c]
+            far_spread(j, source)
+
+    def far_ready(j):
+        for step in range(1, n_wa):
+            source = lax.rem(at_wa + step, n_wa)
+            for part in range(n_ha):
+                far_y(j, source, part, source).wait_recv()
+
+    def far_pair(j):
+        far_ready(j)
+        far_d(j, 1).start()
+
+    def norm_rows(p, c, at):
+        x = stream[p // 2, c, at]
         scale = lax.rsqrt(jnp.mean(x * x, axis=-1, keepdims=True) + EPS)
-        gath[p, me, c] = (x * scale * gain[p:p + 1, :]).astype(BF16)
-
-    def ag_copy(p, slot, c):
+        gath[p, me, c, at] = (x * scale * gain[p:p + 1, :]).astype(BF16)
+
+    def rows_of(part):
+        start = part * part_rows
+        return pl.ds(start if isinstance(part, int) else pl.multiple_of(start, part_rows), part_rows)
+
+    def ag_copy(p, slot, c, part):
         block = me if slot < 2 else remote
         other = remote if slot == 1 else partner
-        ref = gath.at[p, block, c]
-        return remote_copy(ref, ref, ag_s.at[p, slot, c], ag_r.at[p, slot, c], {"ta": other})
-
-    def ag_start(p, c):
-        ag_copy(p, 1, c).start()
-        ag_copy(p, 0, c).start()
+        ref = gath.at[p, block, c, rows_of(part)]
+        return remote_copy(ref, ref, ag_s.at[p, slot, c, part], ag_r.at[p, slot, c, part], {"ta": other})
+
+    def ag_part(p, c, part):
+        ag_copy(p, 1, c, part).start()
+        ag_copy(p, 0, c, part).start()
+
+    def norm_start(p, c):
+        norm_rows(p, c, pl.ds(0, piece))
+        for part in range(n_wa):
+            ag_part(p, c, part)
 
     def ag_wait(p, k, c):
         @pl.when(k == 1)
         def _():
-            ag_copy(p, 0, c).wait_recv()
+            for part in range(n_wa):
+                ag_copy(p, 0, c, part).wait_recv()
 
         @pl.when(k == 2)
         def _():
-            ag_copy(p, 1, c).wait_recv()
-            ag_copy(p, 2, c).start()
+            for part in range(n_wa):
+                ag_copy(p, 1, c, part).wait_recv()
+                ag_copy(p, 2, c, part).start()
 
         @pl.when(k == 3)
         def _():
-            ag_copy(p, 2, c).wait_recv()
+            for part in range(n_wa):
+                ag_copy(p, 2, c, part).wait_recv()
 
     lane_a = lax.broadcasted_iota(jnp.int32, (aw, aw), 0) // HEAD_DIM
     lane_b = lax.broadcasted_iota(jnp.int32, (aw, aw), 1) // HEAD_DIM
@@ -635,36 +666,25 @@
         key_rows = head_norm(flat[:, aw:2 * aw], 2 * p + 1).astype(BF16)
         return queries, key_rows, flat[:, 2 * aw:].astype(BF16)
 
-    def rs_copy(p, slot, c):
-        send, recv = rs_s.at[p, slot, c], rs_r.at[p, slot, c]
-        if slot == 2:
-            return remote_copy(comb.at[p, c], xrec.at[p, c], send, recv, {"ta": remote})
-        return remote_copy(pbuf.at[p, 2 * slot + 1, c], prec.at[p, slot, c], send, recv, {"ta": partner})
-
-    def rs_put(p, k, c, part):
-        pbuf[p, k, c] = part.astype(BF16)
-
-        @pl.when(k == 1)
-        def _():
-            rs_copy(p, 0, c).start()
-
-        @pl.when(k == 3)
-        def _():
-            rs_copy(p, 1, c).start()
-
-    def rs_combine(p, c):
-        rs_copy(p, 1, c).wait_recv()
-        comb[p, c] = (pbuf[p, 2, c].astype(F32) + prec[p, 1, c].astype(F32)).astype(BF16)
-        rs_copy(p, 2, c).start()
-
-    def rs_near(p, c):
-        rs_copy(p, 0, c).wait_recv()
-        return pbuf[p, 0, c].astype(F32) + prec[p, 0, c].astype(F32)
-
-    def rs_total(p, c):
-        near = rs_near(p, c)
-        rs_copy(p, 2, c).wait_recv()
-        return stream[p // 2, c] + (near + xrec[p, c].astype(F32))
+    def lanes_of(block):
+        return pl.ds(pl.multiple_of(block * aw, aw), aw)
+
+    def att_copy(p, c, source, target):
+        return remote_copy(attb.at[p, target, c], att.at[p, c, :, lanes_of(source)],
+                           at_s.at[p, c, target], at_r.at[p, c, source], {"ta": target})
+
+    def rs_copy(c):
+        return remote_copy(pbuf.at[1, c], prec.at[c], rs_s.at[c], rs_r.at[c], {"ta": partner})
+
+    def total_of(p, c):
+        for k in range(1, n_ta):
+            source = block_at(k)
+            att_copy(p, c, source, source).wait_recv()
+        return stream[p // 2, c] + dot(att[p, c], wo[p].reshape(n_ta * aw, model))
+
+    def out_ready(p):
+        for slot in range(2):
+            far_d(p, slot).wait_recv()
 
     def pick_rows(source):
         return (source == lax.broadcasted_iota(jnp.int32, (1, piece), 1)).astype(F32).astype(BF16)
@@ -690,8 +710,8 @@
 
     def x1_send(c):
         w, h, f, r, q = digits(index, (n_wa, n_ha, some_frames, sub_rows, sub_cols))
-        source = number((f, w, r, h, q), (some_frames, n_wa, sub_rows, n_ha, sub_cols))
-        moved = dot(pick_rows(source), rs_total(0, c).astype(BF16)).astype(BF16)
+        source = number((w, f, r, h, q), (n_wa, some_frames, sub_rows, n_ha, sub_cols))
+        moved = dot(pick_rows(source), total_of(0, c).astype(BF16)).astype(BF16)
         sx1[c] = moved.reshape(groups, unit, model)
         for step in range(1, groups):
             x1_copy(c, here, lax.rem(here + step, groups)).start()
@@ -702,15 +722,15 @@
             source = lax.rem(here + step, groups)
             x1_copy(c, source, source).wait_recv()
         stream[0, c] = x1[c].reshape(piece, model).astype(F32)
-        norm_own(1, c)
-        ag_start(1, c)
+        norm_start(1, c)
 
     def fo_copy(c, source, target):
         return remote_copy(fo.at[c, :, :, target], ro.at[c, source], fo_s.at[c, target], fo_r.at[c, source],
                            {"ha": target})
 
     def fo_send(c):
-        near = rs_near(3, c)
+        rs_copy(c).wait_recv()
+        near = pbuf[0, c].astype(F32) + prec[c].astype(F32)
         total = (stream[1, c] + near).astype(BF16)
         fo[c] = total.reshape(CHUNKS, some_wa, n_ha, unit, model)
         for step in range(1, n_ha):
@@ -726,25 +746,36 @@
         moved = dot(pick_rows(source), ro[c].reshape(piece, model)).astype(BF16)
         out[:, c * some_wa:(c + 1) * some_wa] = moved.reshape(frames, some_wa, sub_rows * width, model)
 
-    x0[:, at_wa] = tok[:, at_wa]
     pl.semaphore_wait(barrier, greets)
     for c in range(CHUNKS):
         for step in range(1, n_wa):
             x0_copy(c, at_wa, lax.rem(at_wa + step, n_wa)).start()
-    for j in range(2):
+    far_x(0).start()
+
+    def begin(c, part, tokens):
+        at = rows_of(part)
+        stream[0, c, at] = tokens.reshape(part_rows, model).astype(F32)
+        norm_rows(0, c, at)
+        ag_part(0, c, part)
+
+    for c in range(CHUNKS):
+        begin(c, at_wa, tok[c * some_frames:(c + 1) * some_frames, at_wa])
+    for j in range(3):
+        far_d(j, 0).start()
+    for j in (1, 2):
         far_x(j).start()
     for c in range(CHUNKS):
         for step in range(1, n_wa):
             source = lax.rem(at_wa + step, n_wa)
             x0_copy(c, source, source).wait_recv()
-        stream[0, c] = x0[c * some_frames:(c + 1) * some_frames].reshape(piece, model).astype(F32)
-        norm_own(0, c)
-        ag_start(0, c)
+            begin(c, source, x0[c, source])
+    far_first(0)
+    far_own(0)
 
     column = lax.broadcasted_iota(jnp.int32, (1, piece), 1)
 
     def lines_0(at):
-        f, w, r, q = digits(at, (some_frames, n_wa, sub_rows, width))
+        w, f, r, q = digits(at, (n_wa, some_frames, sub_rows, width))
         return f * sub_rows + r
 
     def lines_1(at):
@@ -756,59 +787,71 @@
         b = block_at(k)
         ag_wait(p, k, c)
         queries, key_rows, values = project(p, b, c)
-        rs_put(p, k, c, dot(attend(queries, key_rows, values, mask), wo[p]))
-
-        @pl.when((k == 2) & (c > 0))
-        def _():
-            rs_combine(p, c - 1)
+        done = attend(queries, key_rows, values, mask)
+
+        @pl.when(k == 0)
+        def _():
+            att[p, c, :, lanes_of(me)] = done
+
+        @pl.when(k > 0)
+        def _():
+            attb[p, b, c] = done
+            att_copy(p, c, me, b).start()
+
+    def after(i, step, actions):
+        @pl.when(i == step)
+        def _():
+            for action, args in actions:
+                action(*args)
+
+    def start_x(j):
+        far_x(j).start()
 
     ready(0)
-    ready(1)
     mask_0 = lines_0(index) == lines_0(column)
 
     def pass_0(i, _):
         line_step(0, i, mask_0)
+        after(i, 1, [(far_next, (0,)), (far_first, (1,))])
+        after(i, 3, [(far_pair, (0,))])
+        after(i, 5, [(start_x, (3,))])
+        after(i, 7, [(start_x, (4,)), (start_x, (5,))])
         return 0
 
     lax.fori_loop(0, steps, pass_0, 0)
-    rs_combine(0, CHUNKS - 1)
-    far_first()
+    ready(1)
+    out_ready(0)
     x1_send(0)
     x1_take(0)
     ready(2)
-    ready(3)
     mask_1 = lines_1(index) == lines_1(column)
 
     def pass_1(i, _):
         for c in range(1, CHUNKS):
-            @pl.when(i == 2 * c - 1)
-            def _():
-                x1_send(c)
-
-            @pl.when(i == 2 * c)
-            def _():
-                x1_take(c)
-
+            after(i, 2 * c - 1, [(x1_send, (c,))])
+            after(i, 2 * c, [(x1_take, (c,))])
+        after(i, 2, [(far_own, (1,)), (far_next, (1,)), (far_first, (2,)), (far_first, (3,))])
+        after(i, 3, [(far_own, (2,)), (far_own, (3,)), (far_first, (4,)), (far_first, (5,))])
+        after(i, 5, [(far_pair, (1,))])
         line_step(1, i, mask_1)
         return 0
 
     lax.fori_loop(0, steps, pass_1, 0)
-    rs_combine(1, CHUNKS - 1)
-    far_next(1)
-
+    ready(3)
+    out_ready(1)
+    far_next(2)
     half_piece = piece // CHUNKS
     for c in range(CHUNKS):
-        total = rs_total(1, c)
+        total = total_of(1, c)
         for d in range(CHUNKS):
             stream[1, d, c * half_piece:(c + 1) * half_piece] = total[d * half_piece:(d + 1) * half_piece]
     for d in range(CHUNKS):
-        norm_own(2, d)
-        ag_start(2, d)
-
+        norm_start(2, d)
     for at in (4, 5):
         ready(at)
-    for step in range(2, n_ha):
-        far_next(step)
+    far_next(3)
+    for j in (4, 5):
+        far_own(j)
     t_i = lax.div(index, unit) * some_frames + lax.div(lax.rem(index, unit), spots)
     t_j = lax.div(column, unit) * some_frames + lax.div(lax.rem(column, unit), spots)
     causal = (lax.rem(index, spots) == lax.rem(column, spots)) & (t_i >= t_j)
@@ -832,18 +875,11 @@
             pk2[c, :, :, g, :, 2 * aw:3 * aw].reshape(piece, aw),
             causal,
         )
-        att2[c, :, :, g] = done.reshape(n_ta, CHUNKS, unit, aw)
-        return 0
-
-    def time_out(i, _):
-        c = lax.div(i, n_ta)
-        k = 3 - lax.rem(i, n_ta)
-        b = block_at(k)
-        rs_put(2, k, c, dot(att2[c, b].reshape(piece, aw), wo[2]))
-
-        @pl.when(k == 1)
-        def _():
-            rs_combine(2, c)
+        for b in range(n_ta):
+            for at in range(CHUNKS):
+                start = (b * CHUNKS + at) * unit
+                rows = pl.ds(pl.multiple_of((at * some_groups + g) * unit, unit), unit)
+                attb[2, b, c, rows] = done[start:start + unit]
         return 0
 
     lax.fori_loop(0, early, time_project, 0)
@@ -851,14 +887,22 @@
     def time_chunk(c, _):
         lax.fori_loop(early + 2 * c, early + 2 * c + 2, time_project, 0)
         lax.fori_loop(c * some_groups, (c + 1) * some_groups, time_attend, 0)
-        lax.fori_loop(c * n_ta, (c + 1) * n_ta, time_out, 0)
+        for k in (2, 3, 1):
+            att_copy(2, c, me, block_at(k)).start()
+        att[2, c, :, lanes_of(me)] = attb[2, me, c]
+
+        @pl.when(c == 0)
+        def _():
+            far_pair(2)
+            far_next(4)
         return 0
 
     lax.fori_loop(0, CHUNKS, time_chunk, 0)
 
     for at in (6, 7):
         ready(at)
-    far_ready()
+    out_ready(2)
+    far_next(5)
     half = wf.shape[0]
 
     def silu_part(x, w_in, w_out):
@@ -874,22 +918,27 @@
         for d in range(CHUNKS):
             @pl.when(i == 2 * d)
             def _():
-                stream[1, d] = rs_total(2, d)
-                norm_own(3, d)
-                ag_copy(3, 0, d).start()
+                stream[1, d] = total_of(2, d)
+                norm_rows(3, d, pl.ds(0, piece))
+                for part in range(n_wa):
+                    ag_copy(3, 0, d, part).start()
+                if d == 0:
+                    for j in (3, 4, 5):
+                        far_ready(j)
 
         @pl.when(k == 1)
         def _():
-            ag_copy(3, 0, c).wait_recv()
+            for part in range(n_wa):
+                ag_copy(3, 0, c, part).wait_recv()
 
         x = gath[3, b, c]
         part = silu_part(x, wi[...], wf[...]) + silu_part(
             x, wi_far[...].reshape(model, 2 * half), wf_far[...].reshape(half, model))
-        pbuf[3, k, c] = part.astype(BF16)
+        pbuf[k, c] = part.astype(BF16)
 
         @pl.when(k == 1)
         def _():
-            rs_copy(3, 0, c).start()
+            rs_copy(c).start()
 
         return 0
 
@@ -906,19 +955,25 @@
             x1_copy(c, here, lax.rem(here + step, groups)).wait_send()
         for step in range(1, n_ha):
             fo_copy(c, at_ha, lax.rem(at_ha + step, n_ha)).wait_send()
+        for part in range(n_wa):
+            for p in range(3):
+                for slot in range(3):
+                    ag_copy(p, slot, c, part).wait_send()
+            ag_copy(3, 0, c, part).wait_send()
         for p in range(3):
-            for slot in range(3):
-                ag_copy(p, slot, c).wait_send()
-                rs_copy(p, slot, c).wait_send()
-        ag_copy(3, 0, c).wait_send()
-        rs_copy(3, 0, c).wait_send()
-    for j in range(2):
+            for k in range(1, n_ta):
+                att_copy(p, c, me, block_at(k)).wait_send()
+        rs_copy(c).wait_send()
+    for j in range(6):
         far_x(j).wait_send()
         for step in range(1, n_ha):
             far_z(j, at_ha, lax.rem(at_ha + step, n_ha)).wait_send()
         for step in range(1, n_wa):
             for part in range(n_ha):
                 far_y(j, at_wa, part, lax.rem(at_wa + step, n_wa)).wait_send()
+    for j in range(3):
+        for slot in range(2):
+            far_d(j, slot).wait_send()
 
 
 def axial_local(sizes, tokens, norm_gain, qkv_weight, qk_gain, out_weight, ffn_in, ffn_out):
@@ -938,42 +993,45 @@
     dma = pltpu.SemaphoreType.DMA
     vm = pltpu.VMEM
     scratch = [
-        vm((frames, n_wa, sub, model), BF16),
+        vm((CHUNKS, n_wa, frames // CHUNKS, sub, model), BF16),
         vm((2, CHUNKS, piece, model), F32),
         vm((4, n_ta, CHUNKS, piece, model), BF16),
         vm((3, model, 3 * aw), BF16),
-        vm((3, aw, model), BF16),
+        vm((3, n_ta, n_wa, n_ha, aw // groups, model), BF16),
         vm((model, 2 * half), BF16),
         vm((half, model), BF16),
-        vm((n_wa, n_ha, model // groups, 2 * half), BF16),
+        vm((2, n_wa, n_ha, model // groups // 2, 2 * half), BF16),
         vm((n_wa, n_ha, half // groups, model), BF16),
         vm((CHUNKS, groups, unit, model), BF16),
         vm((CHUNKS, groups, unit, model), BF16),
         vm((CHUNKS, n_ta, CHUNKS, groups // CHUNKS, unit, 3 * aw), BF16),
-        vm((CHUNKS, n_ta, CHUNKS, groups // CHUNKS, unit, aw), BF16),
-        vm((4, n_ta, CHUNKS, piece, model), BF16),
-        vm((4, 2, CHUNKS, piece, model), BF16),
-        vm((3, CHUNKS, piece, model), BF16),
-        vm((3, CHUNKS, piece, model), BF16),
+        vm((3, n_ta, CHUNKS, piece, aw), BF16),
+        vm((3, CHUNKS, piece, n_ta * aw), BF16),
+        vm((2, CHUNKS, piece, model), BF16),
+        vm((CHUNKS, piece, model), BF16),
         vm((CHUNKS, CHUNKS, n_wa // CHUNKS, n_ha, unit, model), BF16),
         vm((CHUNKS, n_ha, CHUNKS, n_wa // CHUNKS, unit, model), BF16),
         dma((4, 4)),
         dma((CHUNKS, n_wa)),
         dma((CHUNKS, n_wa)),
-        dma((4, 3, CHUNKS)),
-        dma((4, 3, CHUNKS)),
-        dma((4, 3, CHUNKS)),
-        dma((4, 3, CHUNKS)),
+        dma((4, 3, CHUNKS, n_wa)),
+        dma((4, 3, CHUNKS, n_wa)),
+        dma((CHUNKS,)),
+        dma((CHUNKS,)),
+        dma((3, CHUNKS, n_ta)),
+        dma((3, CHUNKS, n_ta)),
         dma((CHUNKS, groups)),
         dma((CHUNKS, groups)),
         dma((CHUNKS, n_ha)),
         dma((CHUNKS, n_ha)),
-        dma((2,)),
-        dma((2,)),
-        dma((2, n_ha)),
-        dma((2, n_ha)),
-        dma((2, n_wa, n_ha)),
-        dma((2, n_wa, n_ha)),
+        dma((6,)),
+        dma((6,)),
+        dma((6, n_ha)),
+        dma((6, n_ha)),
+        dma((6, n_wa, n_ha)),
+        dma((6, n_wa, n_ha)),
+        dma((3, 2)),
+        dma((3, 2)),
     ]
     vmem = pl.BlockSpec(memory_space=pltpu.VMEM)
     anyw = pl.BlockSpec(memory_space=pl.ANY)
@@ -991,7 +1049,7 @@
         norm_gain,
         gains,
         jnp.transpose(qkv_weight, (0, 2, 1, 3)),
-        out_weight,
+        out_weight.reshape(3, n_wa, n_ha, aw // groups, model),
         ffn_in.reshape(model, 2 * half),
         ffn_out,
     )

time: 154 us -> 131 us (0.85)
  Pallas kernels: 147 us -> 124 us
    pallas_call x1, Pallas kernels: 147 us -> 124 us  [axial_local(): pl.pallas_call(functools.partial(axial_kernel, (n_ta, n_ha, n_wa, frames,...]
where the time goes in v2:
time: 131 us; the launch traced here: 130 us
  Pallas kernels  124 us (95%)
  local copies, waits for them, and re-layouts  6.76 us (5%)
    pallas_call x1, Pallas kernels, axial_local(): pl.pallas_call(functools.partial(axial_kernel, (n_ta, n_ha, n_wa, frames,...  124 us
    unnamed x2, local copies, waits for them, and re-layouts  5.38 us

profile of v2, /device:TPU:0, one launch (start us, length us, event | category | flops | bytes accessed | tf_op | source)
XLA Modules:
  0.0 130.3 jit_solution(9322502645186197613)
XLA Ops:
  0.0 0.7 tile.10
  0.7 0.7 tile.12.qkg
  1.4 3.5 %copy.8 = bf16[128,8,2,512]{3,1,2,0:T(8,128)(2,1)} copy(bf16[128,8,2,512]{3,2,1,0:T(2,128)(2,1)} %bitcast.9) | data formatting | bytes 4194304
  4.9 123.6 %axial_layer.1 = bf16[4,2,32,1024]{3,2,1,0:T(8,128)(2,1)} custom-call(bf16[4,2,32,1024]{3,2,1,0:T(8,128)(2,1)} %bitcast.11, f32[4,1024]{1,0:T(4,128)} %gain.1, f32[6,256]{1,0:T(8,128)} %tile.12.qkg, bf16[3,3,1024,256]{3,2,1,0:T(8,128)(2,1)} %bitcast.7, bf16[3,2,4,32,1024]{4,3,2,1,0:T(8,128)(2,1)} %bitcast.10, bf16[1024,1024]{1,0:T(8,128)(2,1)} %bitcast.6, ...), custom_call_target="tpu_custom_call" | custom-call | tf_op jit(solution)/shard_map/axial_layer/pallas_call | solution.py:1038
  128.5 1.9 %copy.10 = bf16[1,4,8,8,1024]{4,3,2,1,0:T(8,128)(2,1)} copy(bf16[1,4,8,8,1024]{4,3,2,1,0:T(8,128)(2,1)} %bitcast.8) | data formatting | bytes 1048576
  (1 shorter events, 0.0 us)

commit v3 on v2

--- a/solution.py
+++ b/solution.py
@@ -476,8 +476,8 @@
 
 def axial_kernel(cfg, tok, gain, qkg, wq_h, wo_h, wi_h, wf_h, out, *s):
     n_ta, n_ha, n_wa, frames, height, width = cfg
-    (x0, stream, gath, wq, wo, wi, wf, wi_far, wf_far, sx1, x1, pk2, attb, att, pbuf, prec, fo, ro,
-     wsem, x0_s, x0_r, ag_s, ag_r, rs_s, rs_r, at_s, at_r, x1_s, x1_r, fo_s, fo_r,
+    (gains, x0, stream, gath, wq, wo, wi, wf, wi_far, wf_far, sx1, x1, pk2, attb, att, pbuf, prec, fo, ro,
+     raw_in, wsem, x0_s, x0_r, ag_s, ag_r, rs_s, rs_r, at_s, at_r, x1_s, x1_r, fo_s, fo_r,
      wx_s, wx_r, wz_s, wz_r, wy_s, wy_r, wd_s, wd_r) = s
     model = tok.shape[-1]
     aw = pk2.shape[-1] // 3
@@ -517,7 +517,7 @@
             pltpu.make_async_copy(wq_h.at[at, j], wq.at[at, :, j * aw:(j + 1) * aw], wsem.at[at, j])
             for j in range(3)])
         copies.append([pltpu.make_async_copy(wo_h.at[at], wo.at[at, me], wsem.at[at, 3])])
-    copies.append([pltpu.make_async_copy(wi_h, wi, wsem.at[3, 0])])
+    copies.append([pltpu.make_async_copy(wi_h, raw_in, wsem.at[3, 0])])
     copies.append([pltpu.make_async_copy(wf_h, wf, wsem.at[3, 1])])
 
     def ready(at):
@@ -540,8 +540,8 @@
             src_ref=src, dst_ref=dst, send_sem=send, recv_sem=recv,
             device_id=place, device_id_type=MESH)
 
-    for group in copies:
-        for copy in group:
+    for at in (6, 0, 1, 2, 3, 4, 5, 7):
+        for copy in copies[at]:
             copy.start()
 
     def x0_copy(c, source, target):
@@ -549,12 +549,20 @@
         return remote_copy(tok.at[at, target], x0.at[c, source], x0_s.at[c, target], x0_r.at[c, source],
                            {"wa": target})
 
-    parts_in = wi_h.shape[0] // wi_far.shape[0]
+    flat_rows = model // 16
+
+    def flatten(i, _):
+        at = pl.ds(pl.multiple_of(i * flat_rows, flat_rows), flat_rows)
+        wi[at] = raw_in[at].reshape(flat_rows, wi.shape[1])
+        return 0
+
+    parts_half = wf_h.shape[0] // n_wa
+    parts_in = model // wi_far.shape[0]
 
     def far(j, shard):
         if j < 3:
             return wo.at[j, shard]
-        return wi_far.at[j - 3] if j < 5 else wf_far
+        return wi_far.at[j - 3]
 
     def far_x(j):
         dst = far(j, me).at[at_wa, at_ha]
@@ -562,9 +570,34 @@
             src = wo_h.at[j, at_wa, at_ha]
         else:
             size = dst.shape[0]
-            first = (j - 3) * parts_in if j < 5 else 0
-            src = (wi_h if j < 5 else wf_h).at[pl.ds(pl.multiple_of(first + here * size, size), size)]
+            first = (j - 3) * parts_in
+            src = wi.at[pl.ds(pl.multiple_of(first + here * size, size), size)]
         return remote_copy(src, dst, wx_s.at[j], wx_r.at[j], {"ta": remote})
+
+    def half_x(part):
+        size = parts_half // n_ha
+        src = wf_h.at[pl.ds(pl.multiple_of(at_wa * parts_half + part * size, size), size)]
+        return remote_copy(src, wf_far.at[at_wa, part], wz_s.at[5, part], wz_r.at[5, part], {"ta": remote})
+
+    def half_y(part, source, target):
+        ref = wf_far.at[source, part]
+        return remote_copy(ref, ref, wy_s.at[5, target, part], wy_r.at[5, source, part], {"wa": target})
+
+    def half_start(first, last):
+        for part in range(first, last):
+            half_x(part).start()
+
+    def half_next(first, last):
+        for part in range(first, last):
+            half_x(part).wait_recv()
+            for step in range(1, n_wa):
+                half_y(part, at_wa, lax.rem(at_wa + step, n_wa)).start()
+
+    def half_ready():
+        for step in range(1, n_wa):
+            source = lax.rem(at_wa + step, n_wa)
+            for part in range(n_ha):
+                half_y(part, source, source).wait_recv()
 
     def far_z(j, source, target):
         ref = far(j, remote).at[at_wa, source]
@@ -592,8 +625,8 @@
     def far_own(j):
         far_spread(j, at_ha)
 
-    def far_next(j):
-        for step in range(1, n_ha):
+    def far_next(j, first, last):
+        for step in range(first, last):
             source = lax.rem(at_ha + step, n_ha)
             far_z(j, source, source).wait_recv()
             far_spread(j, source)
@@ -653,12 +686,13 @@
     lane_b = lax.broadcasted_iota(jnp.int32, (aw, aw), 1) // HEAD_DIM
     ones = (lane_a == lane_b).astype(F32).astype(BF16)
 
+    for p in range(3):
+        gains[2 * p:2 * p + 2, :] = jnp.concatenate([qkg[p]] * (aw // HEAD_DIM), axis=1)
+
     def head_norm(x, row):
         square = x * x
-        high = square.astype(BF16)
-        low = (square - high.astype(F32)).astype(BF16)
-        mean = (dot(high, ones) + dot(low, ones)) * (1.0 / HEAD_DIM)
-        return x * lax.rsqrt(mean + EPS) * qkg[row:row + 1, :]
+        mean = dot(square.astype(BF16), ones) * (1.0 / HEAD_DIM)
+        return x * lax.rsqrt(mean + EPS) * gains[row:row + 1, :]
 
     def project(p, b, c):
         flat = dot(gath[p, b, c], wq[p])
@@ -750,7 +784,8 @@
     for c in range(CHUNKS):
         for step in range(1, n_wa):
             x0_copy(c, at_wa, lax.rem(at_wa + step, n_wa)).start()
-    far_x(0).start()
+    for j in (0, 1):
+        far_x(j).start()
 
     def begin(c, part, tokens):
         at = rows_of(part)
@@ -762,8 +797,9 @@
         begin(c, at_wa, tok[c * some_frames:(c + 1) * some_frames, at_wa])
     for j in range(3):
         far_d(j, 0).start()
-    for j in (1, 2):
-        far_x(j).start()
+    ready(6)
+    lax.fori_loop(0, model // flat_rows, flatten, 0)
+    far_x(3).start()
     for c in range(CHUNKS):
         for step in range(1, n_wa):
             source = lax.rem(at_wa + step, n_wa)
@@ -807,39 +843,46 @@
     def start_x(j):
         far_x(j).start()
 
+    quarter = n_ha // 2
     ready(0)
     mask_0 = lines_0(index) == lines_0(column)
 
     def pass_0(i, _):
         line_step(0, i, mask_0)
-        after(i, 1, [(far_next, (0,)), (far_first, (1,))])
-        after(i, 3, [(far_pair, (0,))])
-        after(i, 5, [(start_x, (3,))])
-        after(i, 7, [(start_x, (4,)), (start_x, (5,))])
+        after(i, 1, [(far_first, (1,)), (far_own, (1,))])
+        after(i, 3, [(far_first, (3,)), (far_own, (3,))])
+        after(i, 5, [(far_next, (0, 1, n_ha))])
+        after(i, 7, [(far_pair, (0,))])
         return 0
 
     lax.fori_loop(0, steps, pass_0, 0)
+    for j in (2, 4):
+        far_x(j).start()
+    half_start(0, quarter)
     ready(1)
     out_ready(0)
-    x1_send(0)
+    for c in range(CHUNKS):
+        x1_send(c)
+    far_next(1, 1, n_ha)
+    far_next(3, 1, n_ha)
     x1_take(0)
     ready(2)
     mask_1 = lines_1(index) == lines_1(column)
 
     def pass_1(i, _):
         for c in range(1, CHUNKS):
-            after(i, 2 * c - 1, [(x1_send, (c,))])
             after(i, 2 * c, [(x1_take, (c,))])
-        after(i, 2, [(far_own, (1,)), (far_next, (1,)), (far_first, (2,)), (far_first, (3,))])
-        after(i, 3, [(far_own, (2,)), (far_own, (3,)), (far_first, (4,)), (far_first, (5,))])
-        after(i, 5, [(far_pair, (1,))])
+        after(i, 2, [(send, (j,)) for j in (2, 4) for send in (far_first, far_own)])
+        after(i, 2, [(half_start, (quarter, n_ha)), (half_next, (0, quarter))])
+        after(i, 4, [(far_pair, (1,))])
         line_step(1, i, mask_1)
         return 0
 
     lax.fori_loop(0, steps, pass_1, 0)
+    far_next(2, 1, n_ha)
+    half_next(quarter, n_ha)
     ready(3)
     out_ready(1)
-    far_next(2)
     half_piece = piece // CHUNKS
     for c in range(CHUNKS):
         total = total_of(1, c)
@@ -849,9 +892,6 @@
         norm_start(2, d)
     for at in (4, 5):
         ready(at)
-    far_next(3)
-    for j in (4, 5):
-        far_own(j)
     t_i = lax.div(index, unit) * some_frames + lax.div(lax.rem(index, unit), spots)
     t_j = lax.div(column, unit) * some_frames + lax.div(lax.rem(column, unit), spots)
     causal = (lax.rem(index, spots) == lax.rem(column, spots)) & (t_i >= t_j)
@@ -883,6 +923,7 @@
         return 0
 
     lax.fori_loop(0, early, time_project, 0)
+    far_next(4, 1, n_ha)
 
     def time_chunk(c, _):
         lax.fori_loop(early + 2 * c, early + 2 * c + 2, time_project, 0)
@@ -894,15 +935,13 @@
         @pl.when(c == 0)
         def _():
             far_pair(2)
-            far_next(4)
+
         return 0
 
     lax.fori_loop(0, CHUNKS, time_chunk, 0)
 
-    for at in (6, 7):
-        ready(at)
+    ready(7)
     out_ready(2)
-    far_next(5)
     half = wf.shape[0]
 
     def silu_part(x, w_in, w_out):
@@ -918,13 +957,12 @@
         for d in range(CHUNKS):
             @pl.when(i == 2 * d)
             def _():
+                if d > 0:
+                    fo_send(d - 1)
                 stream[1, d] = total_of(2, d)
                 norm_rows(3, d, pl.ds(0, piece))
                 for part in range(n_wa):
                     ag_copy(3, 0, d, part).start()
-                if d == 0:
-                    for j in (3, 4, 5):
-                        far_ready(j)
 
         @pl.when(k == 1)
         def _():
@@ -932,8 +970,15 @@
                 ag_copy(3, 0, c, part).wait_recv()
 
         x = gath[3, b, c]
-        part = silu_part(x, wi[...], wf[...]) + silu_part(
-            x, wi_far[...].reshape(model, 2 * half), wf_far[...].reshape(half, model))
+        part = silu_part(x, wi[...], wf[...])
+
+        @pl.when(i == 0)
+        def _():
+            for j in (3, 4):
+                far_ready(j)
+            half_ready()
+
+        part += silu_part(x, wi_far[...].reshape(model, 2 * half), wf_far[...].reshape(half, model))
         pbuf[k, c] = part.astype(BF16)
 
         @pl.when(k == 1)
@@ -943,8 +988,7 @@
         return 0
 
     lax.fori_loop(0, 2 * CHUNKS, mlp, 0)
-    for c in range(CHUNKS):
-        fo_send(c)
+    fo_send(CHUNKS - 1)
     for c in range(CHUNKS):
         fo_take(c)
 
@@ -964,7 +1008,11 @@
             for k in range(1, n_ta):
                 att_copy(p, c, me, block_at(k)).wait_send()
         rs_copy(c).wait_send()
-    for j in range(6):
+    for part in range(n_ha):
+        half_x(part).wait_send()
+        for step in range(1, n_wa):
+            half_y(part, at_wa, lax.rem(at_wa + step, n_wa)).wait_send()
+    for j in range(5):
         far_x(j).wait_send()
         for step in range(1, n_ha):
             far_z(j, at_ha, lax.rem(at_ha + step, n_ha)).wait_send()
@@ -988,11 +1036,10 @@
     groups = n_ha * n_wa
     unit = piece // groups
     sub = height // n_wa * width
-    heads = aw // HEAD_DIM
-    gains = jnp.tile(qk_gain.reshape(-1, HEAD_DIM), (1, heads))
     dma = pltpu.SemaphoreType.DMA
     vm = pltpu.VMEM
     scratch = [
+        vm((6, aw), F32),
         vm((CHUNKS, n_wa, frames // CHUNKS, sub, model), BF16),
         vm((2, CHUNKS, piece, model), F32),
         vm((4, n_ta, CHUNKS, piece, model), BF16),
@@ -1011,6 +1058,7 @@
         vm((CHUNKS, piece, model), BF16),
         vm((CHUNKS, CHUNKS, n_wa // CHUNKS, n_ha, unit, model), BF16),
         vm((CHUNKS, n_ha, CHUNKS, n_wa // CHUNKS, unit, model), BF16),
+        vm((model, 2, half), BF16),
         dma((4, 4)),
         dma((CHUNKS, n_wa)),
         dma((CHUNKS, n_wa)),
@@ -1047,10 +1095,10 @@
     )(
         tokens.reshape(frames, n_wa, sub, model),
         norm_gain,
-        gains,
+        qk_gain,
         jnp.transpose(qkv_weight, (0, 2, 1, 3)),
         out_weight.reshape(3, n_wa, n_ha, aw // groups, model),
-        ffn_in.reshape(model, 2 * half),
+        ffn_in,
         ffn_out,
     )
     return result.reshape(extent)

time: 131 us -> 109 us (0.83)
  Pallas kernels: 124 us -> 107 us
  local copies, waits for them, and re-layouts: 6.76 us -> 1.87 us
    pallas_call x1, Pallas kernels: 124 us -> 107 us  [axial_local(): pl.pallas_call(functools.partial(axial_kernel, (n_ta, n_ha, n_wa, frames,...]
    unnamed x2 -> x1, local copies, waits for them, and re-layouts: 5.38 us -> 1.87 us
    another operation x3 -> x0, local copies, waits for them, and re-layouts: 1.38 us -> none  [axial_local(): gains = jnp.tile(qk_gain.reshape(-1, HEAD_DIM), (1, heads))]
where the time goes in v3:
time: 109 us
  Pallas kernels  107 us (98%)
  local copies, waits for them, and re-layouts  1.87 us (2%)
    pallas_call x1, Pallas kernels, axial_local(): pl.pallas_call(functools.partial(axial_kernel, (n_ta, n_ha, n_wa, frames,...  107 us

profile of v3, /device:TPU:0, one launch (start us, length us, event | category | flops | bytes accessed | tf_op | source)
XLA Modules:
  0.0 109.0 jit_solution(8596287525466661113)
XLA Ops:
  0.0 107.1 %axial_layer.1 = bf16[4,2,32,1024]{3,2,1,0:T(8,128)(2,1)} custom-call(bf16[4,2,32,1024]{3,2,1,0:T(8,128)(2,1)} %bitcast.7, f32[4,1024]{1,0:T(4,128)} %gain.1, f32[3,2,64]{2,1,0:T(2,128)} %qkg.1, bf16[3,3,1024,256]{3,2,1,0:T(8,128)(2,1)} %bitcast.4, bf16[3,2,4,32,1024]{4,3,2,1,0:T(8,128)(2,1)} %bitcast.6, bf16[1024,2,512]{2,1,0:T(2,128)(2,1)} %wi_h.1, ...), custom_call_target="tpu_custom_call" | custom-call | tf_op jit(solution)/shard_map/axial_layer/pallas_call | solution.py:1086
  107.1 1.9 %copy.9 = bf16[1,4,8,8,1024]{4,3,2,1,0:T(8,128)(2,1)} copy(bf16[1,4,8,8,1024]{4,3,2,1,0:T(8,128)(2,1)} %bitcast.5) | data formatting | bytes 1048576

commit v4 on v3

--- a/solution.py
+++ b/solution.py
@@ -784,8 +784,7 @@
     for c in range(CHUNKS):
         for step in range(1, n_wa):
             x0_copy(c, at_wa, lax.rem(at_wa + step, n_wa)).start()
-    for j in (0, 1):
-        far_x(j).start()
+    far_x(0).start()
 
     def begin(c, part, tokens):
         at = rows_of(part)
@@ -797,15 +796,15 @@
         begin(c, at_wa, tok[c * some_frames:(c + 1) * some_frames, at_wa])
     for j in range(3):
         far_d(j, 0).start()
+    far_x(1).start()
     ready(6)
     lax.fori_loop(0, model // flat_rows, flatten, 0)
-    far_x(3).start()
+    far_first(0)
     for c in range(CHUNKS):
         for step in range(1, n_wa):
             source = lax.rem(at_wa + step, n_wa)
             x0_copy(c, source, source).wait_recv()
             begin(c, source, x0[c, source])
-    far_first(0)
     far_own(0)
 
     column = lax.broadcasted_iota(jnp.int32, (1, piece), 1)
@@ -849,22 +848,20 @@
 
     def pass_0(i, _):
         line_step(0, i, mask_0)
-        after(i, 1, [(far_first, (1,)), (far_own, (1,))])
-        after(i, 3, [(far_first, (3,)), (far_own, (3,))])
-        after(i, 5, [(far_next, (0, 1, n_ha))])
-        after(i, 7, [(far_pair, (0,))])
+        after(i, 3, [(far_first, (1,)), (far_own, (1,)), (start_x, (3,))])
+        after(i, 4, [(far_next, (0, 1, n_ha))])
         return 0
 
     lax.fori_loop(0, steps, pass_0, 0)
     for j in (2, 4):
         far_x(j).start()
     half_start(0, quarter)
+    far_pair(0)
     ready(1)
     out_ready(0)
     for c in range(CHUNKS):
         x1_send(c)
     far_next(1, 1, n_ha)
-    far_next(3, 1, n_ha)
     x1_take(0)
     ready(2)
     mask_1 = lines_1(index) == lines_1(column)
@@ -872,15 +869,16 @@
     def pass_1(i, _):
         for c in range(1, CHUNKS):
             after(i, 2 * c, [(x1_take, (c,))])
-        after(i, 2, [(send, (j,)) for j in (2, 4) for send in (far_first, far_own)])
+        after(i, 2, [(far_first, (3,)), (far_own, (3,))])
         after(i, 2, [(half_start, (quarter, n_ha)), (half_next, (0, quarter))])
         after(i, 4, [(far_pair, (1,))])
+        after(i, 5, [(far_first, (2,)), (far_own, (2,))])
+        after(i, 7, [(far_first, (4,)), (far_own, (4,))])
         line_step(1, i, mask_1)
         return 0
 
     lax.fori_loop(0, steps, pass_1, 0)
-    far_next(2, 1, n_ha)
-    half_next(quarter, n_ha)
+    far_next(3, 1, n_ha)
     ready(3)
     out_ready(1)
     half_piece = piece // CHUNKS
@@ -890,6 +888,8 @@
             stream[1, d, c * half_piece:(c + 1) * half_piece] = total[d * half_piece:(d + 1) * half_piece]
     for d in range(CHUNKS):
         norm_start(2, d)
+    half_next(quarter, n_ha)
+    far_next(2, 1, n_ha)
     for at in (4, 5):
         ready(at)
     t_i = lax.div(index, unit) * some_frames + lax.div(lax.rem(index, unit), spots)
@@ -923,10 +923,14 @@
         return 0
 
     lax.fori_loop(0, early, time_project, 0)
-    far_next(4, 1, n_ha)
 
     def time_chunk(c, _):
         lax.fori_loop(early + 2 * c, early + 2 * c + 2, time_project, 0)
+
+        @pl.when(c == 0)
+        def _():
+            far_next(4, 1, n_ha)
+
         lax.fori_loop(c * some_groups, (c + 1) * some_groups, time_attend, 0)
         for k in (2, 3, 1):
             att_copy(2, c, me, block_at(k)).start()

time: 109 us -> 108 us (level)
    pallas_call x1, Pallas kernels: 107 us -> 106 us  [axial_local(): pl.pallas_call(functools.partial(axial_kernel, (n_ta, n_ha, n_wa, frames,...]
where the time goes in v4:
time: 108 us
  Pallas kernels  106 us (98%)
  local copies, waits for them, and re-layouts  1.87 us (2%)
    pallas_call x1, Pallas kernels, axial_local(): pl.pallas_call(functools.partial(axial_kernel, (n_ta, n_ha, n_wa, frames,...  106 us

profile of v4, /device:TPU:0, one launch (start us, length us, event | category | flops | bytes accessed | tf_op | source)
XLA Modules:
  0.0 107.8 jit_solution(7790593524243527574)
XLA Ops:
  0.0 105.9 %axial_layer.1 = bf16[4,2,32,1024]{3,2,1,0:T(8,128)(2,1)} custom-call(bf16[4,2,32,1024]{3,2,1,0:T(8,128)(2,1)} %bitcast.7, f32[4,1024]{1,0:T(4,128)} %gain.1, f32[3,2,64]{2,1,0:T(2,128)} %qkg.1, bf16[3,3,1024,256]{3,2,1,0:T(8,128)(2,1)} %bitcast.4, bf16[3,2,4,32,1024]{4,3,2,1,0:T(8,128)(2,1)} %bitcast.6, bf16[1024,2,512]{2,1,0:T(2,128)(2,1)} %wi_h.1, ...), custom_call_target="tpu_custom_call" | custom-call | tf_op jit(solution)/shard_map/axial_layer/pallas_call | solution.py:1090
  105.9 1.9 %copy.9 = bf16[1,4,8,8,1024]{4,3,2,1,0:T(8,128)(2,1)} copy(bf16[1,4,8,8,1024]{4,3,2,1,0:T(8,128)(2,1)} %bitcast.5) | data formatting | bytes 1048576
